TPU v7x, 32 devices: a whole 2x2x4 slice. The times are simulated.
32 devices in a mesh: dp: 8 (over y, x, core), seq: 4 (over z).
Axes of the slice: x: 2, y: 2, z: 4, core: 2. Of those that a mesh axis runs over, the one named last changes fastest.
Arguments:
- inputs: bfloat16 [24, 1024, 768], P('dp', 'seq'), may hold values from -6 to 6
- segments: int32 [24, 1024], P('dp'), may hold values from 0 to 3, never falling along the last dimension, each value on 1 to 512 neighbouring positions
- cotangent: bfloat16 [24, 1024, 768], P('dp', 'seq'), may hold values from -6 to 6
- weights: float32 [768, 9216], P(None, 'dp'), may hold values from -0.18042196 to 0.18042196
- first_moment: float32 [768, 9216], P(None, 'dp'), may hold values from -112 to 112
- second_moment: float32 [768, 9216], P(None, 'dp'), may hold values from 12.288 to 98.304
- bases: float32 [4, 768, 768], replicated, may hold values from -0.08660254 to 0.8866025
- right_bases: float32 [9216, 3072], P('dp'), may hold values from -0.08660254 to 0.8866025, as said below
- small: float32 [9216], replicated, may hold values from -2 to 2
- small_first: float32 [9216], replicated, may hold values from -112 to 112
- small_second: float32 [9216], replicated, may hold values from 12.288 to 98.304
Outputs:
- output: bfloat16 [24, 1024, 768], P('dp', 'seq')
- input_grad: bfloat16 [24, 1024, 768], P('dp', 'seq')
- weight_grad: float32 [768, 9216], P(None, 'dp')
- first_new: float32 [768, 9216], P(None, 'dp')
- second_new: float32 [768, 9216], P(None, 'dp')
- weights_new: float32 [768, 9216], P(None, 'dp')
- weights_low: bfloat16 [768, 9216], P(None, 'dp')
- small_grad: float32 [9216], replicated
- small_first_new: float32 [9216], replicated
- small_second_new: float32 [9216], replicated
- small_new: float32 [9216], replicated
Inputs may be any that keep to these rules, and one draw needn't show every extreme that they name: `segments`: along each row the ids never fall; every id covers 1 to 512 positions and one covers exactly 512. `right_bases`: entries of a row past the number of columns of that row's block are zero.
All inputs are finite; a program needn't handle non-finite values.
Results may differ from a plain program's by a relative error of at most 0.012.
Values may be sent and summed in bfloat16 or wider, within the bound.
A program may use at most 256 MiB of HBM per device.

v0:
```python
import jax
import jax.numpy as jnp
from jax import lax
from jax.sharding import PartitionSpec as P

D = 768
HEADS = 12
HD = 64
FF = 3072
STEP = 10
highest = lax.Precision.HIGHEST
norm_eps = 1e-12
beta_first = 0.9
beta_second = 0.999
adam_eps = 1e-08
learn_rate = 0.03
small_rate = 0.3


def contract_first(left, right):
    return lax.dot_general(
        left, right, (((0,), (0,)), ((), ())), preferred_element_type=jnp.float32
    )


def contract_last(left, right):
    return lax.dot_general(
        left, right, (((1,), (1,)), ((), ())), preferred_element_type=jnp.float32
    )


def exact_last(left, right):
    return lax.dot_general(
        left, right, (((1,), (1,)), ((), ())), precision=highest, preferred_element_type=jnp.float32
    )


def normalize(resid, gain, shift):
    centre = resid - jnp.mean(resid, axis=-1, keepdims=True)
    spread = jnp.mean(centre * centre, axis=-1, keepdims=True)
    inv_std = lax.rsqrt(spread + norm_eps)
    scaled = centre * inv_std
    return (scaled * gain + shift, scaled, inv_std)


def norm_back(grad, scaled, inv_std, gain):
    lifted = grad * gain
    return inv_std * (
        lifted
        - jnp.mean(lifted, axis=-1, keepdims=True)
        - scaled * jnp.mean(lifted * scaled, axis=-1, keepdims=True)
    )


def moments(grad, first, second):
    first_out = beta_first * first + (1.0 - beta_first) * grad
    second_out = beta_second * second + (1.0 - beta_second) * grad * grad
    heading = (
        first_out
        / (1.0 - beta_first**STEP)
        / (jnp.sqrt(second_out / (1.0 - beta_second**STEP)) + adam_eps)
    )
    return (first_out, second_out, heading)


def on_device(
    inputs,
    segments,
    cotangent,
    weights,
    first_moment,
    second_moment,
    bases,
    right_bases,
    small,
    small_first,
    small_second,
):
    number, quarter, width = inputs.shape
    length = segments.shape[1]
    groups = lax.axis_size("seq")
    owners = lax.axis_size("dp")
    heads_local = HEADS // groups
    group_width = width // groups
    scale = HD ** (-0.5)
    share = weights.shape[1]
    block_widths = [3 * D // owners, D // owners, FF // owners, FF // owners]
    block_starts = [
        0,
        block_widths[0],
        block_widths[0] + block_widths[1],
        block_widths[0] + block_widths[1] + block_widths[2],
    ]

    def split_wide(matrix):
        shaped = matrix.reshape(matrix.shape[0], owners, share)
        return [
            shaped[:, :, block_starts[which] : block_starts[which] + block_widths[which]].reshape(
                matrix.shape[0], owners * block_widths[which]
            )
            for which in range(4)
        ]

    def join_wide(parts):
        rows = parts[0].shape[0]
        return jnp.concatenate(
            [parts[which].reshape(rows, owners, block_widths[which]) for which in range(4)], axis=2
        ).reshape(rows, owners * share)

    wide = lax.all_gather(weights.astype(jnp.bfloat16), "dp", axis=1, tiled=True)
    w_qkv, w_out, w_up, w_down = split_wide(wide)
    pieces = [small[index * D : (index + 1) * D] for index in range(8)] + [small[8 * D :]]
    (
        gain_one,
        gain_two,
        shift_one,
        shift_two,
        bias_query,
        bias_value,
        bias_out,
        bias_down,
        bias_up,
    ) = pieces
    token_rows = inputs.reshape(number * quarter, width)
    acts = token_rows.astype(jnp.float32)
    project = jnp.dot(token_rows, w_qkv, preferred_element_type=jnp.float32)
    queries = (project[:, :D] + bias_query).astype(jnp.bfloat16)
    keys_all = project[:, D : 2 * D].astype(jnp.bfloat16)
    values = (project[:, 2 * D :] + bias_value).astype(jnp.bfloat16)

    def to_heads(array):
        return array.reshape(number, quarter, groups, group_width)

    head_q, head_k, head_v = (
        lax.all_to_all(to_heads(queries), "seq", split_axis=2, concat_axis=1, tiled=True),
        lax.all_to_all(to_heads(keys_all), "seq", split_axis=2, concat_axis=1, tiled=True),
        lax.all_to_all(to_heads(values), "seq", split_axis=2, concat_axis=1, tiled=True),
    )
    head_q = head_q.reshape(number, length, heads_local, HD)
    head_k = head_k.reshape(number, length, heads_local, HD)
    head_v = head_v.reshape(number, length, heads_local, HD)

    def attend_one(item):
        one_q, one_k, one_v, marks = item
        same = (marks[:, None] == marks[None, :])[None]
        raw = jnp.einsum("qhd,khd->hqk", one_q, one_k, preferred_element_type=jnp.float32) * scale
        masked = jnp.where(same, raw, -1e30)
        peak = jnp.max(masked, axis=-1, keepdims=True)
        expo = jnp.exp(masked - peak)
        totals = jnp.sum(expo, axis=-1, keepdims=True)
        probs = expo / totals
        log_sum = peak + jnp.log(totals)
        mixed = jnp.einsum(
            "hqk,khd->qhd", probs.astype(jnp.bfloat16), one_v, preferred_element_type=jnp.float32
        )
        return (mixed.astype(jnp.bfloat16), log_sum)

    mixed, log_sums = lax.map(attend_one, (head_q, head_k, head_v, segments))
    context_heads = mixed.reshape(number, length, 1, group_width)
    context = lax.all_to_all(context_heads, "seq", split_axis=1, concat_axis=2, tiled=True).reshape(
        number * quarter, width
    )
    attended = jnp.dot(context, w_out, preferred_element_type=jnp.float32) + bias_out
    first, scaled_one, inv_one = normalize(acts + attended, gain_one, shift_one)
    first_low = first.astype(jnp.bfloat16)
    upward = jnp.dot(first_low, w_up, preferred_element_type=jnp.float32) + bias_up
    active_full, gelu_pull = jax.vjp(lambda value: jax.nn.gelu(value, approximate=False), upward)
    active = active_full.astype(jnp.bfloat16)
    downward = contract_last(active, w_down) + bias_down
    output, scaled_two, inv_two = normalize(first + downward, gain_two, shift_two)
    grad_out = cotangent.reshape(number * quarter, width).astype(jnp.float32)
    d_two = norm_back(grad_out, scaled_two, inv_two, gain_two)
    grad_gain_two = jnp.sum(grad_out * scaled_two, axis=0)
    grad_shift_two = jnp.sum(grad_out, axis=0)
    d_down = d_two.astype(jnp.bfloat16)
    grad_bias_down = jnp.sum(d_down.astype(jnp.float32), axis=0)
    grad_w_down = contract_first(d_down, active)
    d_active = jnp.dot(d_down, w_down, preferred_element_type=jnp.float32)
    (d_up_full,) = gelu_pull(d_active)
    d_up = d_up_full.astype(jnp.bfloat16)
    grad_bias_up = jnp.sum(d_up.astype(jnp.float32), axis=0)
    grad_w_up = contract_first(first_low, d_up)
    d_first = d_two + contract_last(d_up, w_up)
    d_one = norm_back(d_first, scaled_one, inv_one, gain_one)
    grad_gain_one = jnp.sum(d_first * scaled_one, axis=0)
    grad_shift_one = jnp.sum(d_first, axis=0)
    d_att = d_one.astype(jnp.bfloat16)
    grad_bias_out = jnp.sum(d_att.astype(jnp.float32), axis=0)
    grad_w_out = contract_first(context, d_att)
    d_context = contract_last(d_att, w_out).astype(jnp.bfloat16)
    d_heads = lax.all_to_all(
        to_heads(d_context), "seq", split_axis=2, concat_axis=1, tiled=True
    ).reshape(number, length, heads_local, HD)

    def attend_back(item):
        one_q, one_k, one_v, marks, one_grad, one_log = item
        same = (marks[:, None] == marks[None, :])[None]
        raw = jnp.einsum("qhd,khd->hqk", one_q, one_k, preferred_element_type=jnp.float32) * scale
        again = jnp.where(same, jnp.exp(raw - one_log), 0.0)
        d_values = jnp.einsum(
            "hqk,qhd->khd", again.astype(jnp.bfloat16), one_grad, preferred_element_type=jnp.float32
        )
        d_probs = jnp.einsum("qhd,khd->hqk", one_grad, one_v, preferred_element_type=jnp.float32)
        d_scores = (again * (d_probs - jnp.sum(again * d_probs, axis=-1, keepdims=True))).astype(
            jnp.bfloat16
        )
        d_queries = (
            jnp.einsum("hqk,khd->qhd", d_scores, one_k, preferred_element_type=jnp.float32) * scale
        )
        d_keys = (
            jnp.einsum("hqk,qhd->khd", d_scores, one_q, preferred_element_type=jnp.float32) * scale
        )
        return (
            d_queries.astype(jnp.bfloat16),
            d_keys.astype(jnp.bfloat16),
            d_values.astype(jnp.bfloat16),
        )

    grads_q, grads_k, grads_v = lax.map(
        attend_back, (head_q, head_k, head_v, segments, d_heads, log_sums)
    )

    def to_send(array):
        return array.reshape(number, length, 1, group_width)

    back_q, back_k, back_v = (
        lax.all_to_all(to_send(grads_q), "seq", split_axis=1, concat_axis=2, tiled=True),
        lax.all_to_all(to_send(grads_k), "seq", split_axis=1, concat_axis=2, tiled=True),
        lax.all_to_all(to_send(grads_v), "seq", split_axis=1, concat_axis=2, tiled=True),
    )
    d_project = jnp.concatenate(
        [
            back_q.reshape(number * quarter, width),
            back_k.reshape(number * quarter, width),
            back_v.reshape(number * quarter, width),
        ],
        axis=1,
    )
    grad_bias_query = jnp.sum(back_q.reshape(number * quarter, width).astype(jnp.float32), axis=0)
    grad_bias_value = jnp.sum(back_v.reshape(number * quarter, width).astype(jnp.float32), axis=0)
    grad_w_qkv = contract_first(token_rows, d_project)
    input_grad = (d_one + contract_last(d_project, w_qkv)).astype(jnp.bfloat16)
    grad_full = join_wide([grad_w_qkv, grad_w_out, grad_w_up, grad_w_down])
    small_local = jnp.concatenate(
        [
            grad_gain_one,
            grad_gain_two,
            grad_shift_one,
            grad_shift_two,
            grad_bias_query,
            grad_bias_value,
            grad_bias_out,
            grad_bias_down,
            grad_bias_up,
        ]
    )
    small_grad = lax.psum(small_local, ("dp", "seq"))
    reduced = lax.psum_scatter(grad_full, "dp", scatter_dimension=1, tiled=True)
    reduced = lax.psum(reduced.astype(jnp.bfloat16), "seq").astype(jnp.float32)
    right_rows = []
    turned_parts = []
    for which in range(4):
        begin = block_starts[which]
        count = block_widths[which]
        extent = owners * count
        rows_here = right_bases[begin : begin + count, :extent]
        right_rows.append(rows_here)
        left_turned = jnp.dot(bases[which].T, reduced[:, begin : begin + count], precision=highest)
        turned_parts.append(jnp.dot(left_turned, rows_here, precision=highest))
    term = join_wide(turned_parts)
    rotated = lax.psum_scatter(term, "dp", scatter_dimension=1, tiled=True)
    first_new, second_new, heading = moments(rotated, first_moment, second_moment)
    left_step = jnp.concatenate(
        [
            jnp.dot(
                bases[which],
                heading[:, block_starts[which] : block_starts[which] + block_widths[which]],
                precision=highest,
            )
            for which in range(4)
        ],
        axis=1,
    )
    every_step = lax.all_gather(left_step.astype(jnp.bfloat16), "dp", axis=1, tiled=True).astype(
        left_step.dtype
    )
    step_parts = split_wide(every_step)
    update = jnp.concatenate(
        [exact_last(step_parts[which], right_rows[which]) for which in range(4)], axis=1
    )
    weights_new = weights - learn_rate * update
    small_first_new, small_second_new, small_heading = moments(
        small_grad, small_first, small_second
    )
    small_new = small - small_rate * small_heading
    return (
        output.astype(jnp.bfloat16).reshape(number, quarter, width),
        input_grad.reshape(number, quarter, width),
        reduced,
        first_new,
        second_new,
        weights_new,
        weights_new.astype(jnp.bfloat16),
        small_grad,
        small_first_new,
        small_second_new,
        small_new,
    )


def solution(mesh):
    return jax.shard_map(
        on_device,
        mesh=mesh,
        in_specs=(
            P("dp", "seq", None),
            P("dp", None),
            P("dp", "seq", None),
            P(None, "dp"),
            P(None, "dp"),
            P(None, "dp"),
            P(),
            P("dp", None),
            P(),
            P(),
            P(),
        ),
        out_specs=(
            P("dp", "seq", None),
            P("dp", "seq", None),
            P(None, "dp"),
            P(None, "dp"),
            P(None, "dp"),
            P(None, "dp"),
            P(None, "dp"),
            P(),
            P(),
            P(),
            P(),
        ),
        check_vma=False,
    )
```

profile of v0, /device:TPU:0, one launch (start us, length us, event | category | flops | bytes accessed | tf_op | source)
XLA Modules:
  0.0 1506.3 jit_solution(18342674644949686309)
XLA Ops:
  11.3 80.8 %all-gather.3.cloned.1.call-done = bf16[768,9216]{1,0:T(8,128)(2,1)} async-done(((bf16[768,1152]{1,0:T(8,128)(2,1)}), bf16[768,9216]{1,0:T(8,128)(2,1)}) %all-gather.3.cloned.1.call-update) | async-done | bytes 14155792 | tf_op jit(solution)/shard_map/all_gather | solution.py:110
  92.1 18.5 %copy.112 = bf16[768,9216]{0,1:T(8,128)(2,1)} copy(bf16[768,9216]{1,0:T(8,128)(2,1)} %all-gather.3.cloned.1.call-done) | data formatting | bytes 28311552 | tf_op jit(solution)/shard_map/all_gather | solution.py:110
  132.9 23.3 %all-to-all-done = bf16[3,256,4,192]{1,3,0,2:T(8,128)(2,1)S(1)} async-done(((bf16[3,256,4,192]{1,3,0,2:T(8,128)(2,1)}), bf16[3,256,4,192]{1,3,0,2:T(8,128)(2,1)S(1)}, u32[]{:S(2)}, u32[]{:S(2)}) %all-to-all-start) | async-done | bytes 1179680 | tf_op jit(solution)/shard_map/all_to_all | solution.py:137
  168.9 19.7 %all-to-all-done.1 = bf16[3,256,4,192]{1,3,0,2:T(8,128)(2,1)} async-done(((bf16[3,256,4,192]{1,3,0,2:T(8,128)(2,1)}), bf16[3,256,4,192]{1,3,0,2:T(8,128)(2,1)}, u32[]{:S(2)}, u32[]{:S(2)}) %all-to-all-start.1) | async-done | bytes 1179680 | tf_op jit(solution)/shard_map/all_to_all | solution.py:135
  201.9 18.8 %all-to-all-done.2 = bf16[3,256,4,192]{1,3,0,2:T(8,128)(2,1)S(1)} async-done(((bf16[3,256,4,192]{1,3,0,2:T(8,128)(2,1)}), bf16[3,256,4,192]{1,3,0,2:T(8,128)(2,1)S(1)}, u32[]{:S(2)}, u32[]{:S(2)}) %all-to-all-start.2) | async-done | bytes 1179680 | tf_op jit(solution)/shard_map/all_to_all | solution.py:136
  224.5 47.5 %while.26 = (s32[]{:T(128)}, bf16[3,1024,3,64]{1,3,2,0:T(8,128)(2,1)}, f32[3,3,1024,1]{2,1,3,0:T(4,128)}, bf16[3,1024,3,64]{1,3,2,0:T(8,128)(2,1)}, s32[3,1024]{...) while((s32[]{:T(128)}, ...), condition=%wide.region_3.4_spmd, body=%wide.region_0.3_spmd.sunk | while | flops 844297216 | bytes 47827072 | solution.py:158
  293.1 35.5 %all-to-all-done.3 = bf16[3,1024,1,192]{3,0,2,1:T(4,128)(2,1)} async-done(((bf16[3,1024,1,192]{3,0,2,1:T(4,128)(2,1)}), bf16[3,1024,1,192]{3,0,2,1:T(4,128)(2,1)}, u32[]{:S(2)}, u32[]{:S(2)}) %all-to-all-start.3) | async-done | bytes 1179680 | tf_op jit(solution)/shard_map/all_to_all | solution.py:160
  342.1 28.3 %multiply_convert_fusion.1 = (bf16[768,3072]{1,0:T(8,128)(2,1)S(1)}, f32[768,3072]{1,0:T(8,128)}, f32[768,3072]{1,0:T(8,128)}) fusion(f32[3072]{0:T(1024)S(1)} %slice.124, bf16[768,3072]{0,1:T(8,128)(2,1)} %bitcast.308, f32[768,768]{1,0:T(8,128)S(1)} %get-tuple-element.239, f32[768]{0:T(1024)S(1)} %copy-done.32, f32[768]{0:T(1024)S(1)} %copy-done.28, ...), kind=kOutput, calls=%fused_computation.70 | convolution fusion | flops 3782541312 | bytes 30695424 | tf_op jit(solution)/shard_map/dot_general | solution.py:166
  379.0 13.2 convert_reduce_fusion
  404.9 30.7 %all_to_all.120 = bf16[3,256,4,192]{1,3,0,2:T(8,128)(2,1)S(1)} all-to-all(bf16[3,256,4,192]{1,3,0,2:T(8,128)(2,1)S(1)} %copy.122), channel_id=1, replica_groups=mesh['dp'=8,'seq'=4] {'seq'}, dimensions={2} | all-to-all | bytes 2359296 | tf_op jit(solution)/shard_map/all_to_all | solution.py:191
  443.9 81.4 %while.27 = (s32[]{:T(128)}, bf16[3,1024,3,64]{1,3,2,0:T(8,128)(2,1)}, bf16[3,1024,3,64]{1,3,2,0:T(8,128)(2,1)}, bf16[3,1024,3,64]{1,3,2,0:T(8,128)(2,1)}, bf16[...) while((s32[]{:T(128)}, ...), condition=%wide.region_14.15_spmd, body=%wide.region_12.14_spmd.sunk | while | flops 2062480384 | bytes 102610048 | solution.py:219
  536.4 44.7 %all-to-all-done.5 = bf16[3,1024,1,192]{3,0,2,1:T(4,128)(2,1)} async-done(((bf16[3,1024,1,192]{3,0,2,1:T(4,128)(2,1)}), bf16[3,1024,1,192]{3,0,2,1:T(4,128)(2,1)}, u32[]{:S(2)}, u32[]{:S(2)}) %all-to-all-start.5) | async-done | bytes 1179680 | tf_op jit(solution)/shard_map/all_to_all | solution.py:227
  598.0 35.8 %all-to-all-done.6 = bf16[3,1024,1,192]{3,0,2,1:T(4,128)(2,1)} async-done(((bf16[3,1024,1,192]{3,0,2,1:T(4,128)(2,1)}), bf16[3,1024,1,192]{3,0,2,1:T(4,128)(2,1)}, u32[]{:S(2)}, u32[]{:S(2)}) %all-to-all-start.6) | async-done | bytes 1179680 | tf_op jit(solution)/shard_map/all_to_all | solution.py:228
  716.1 30.4 %concatenate.20 = f32[768,8,1152]{2,1,0:T(8,128)} concatenate(f32[768,8,288]{2,1,0:T(8,128)} %copy.134, f32[768,8,96]{2,1,0:T(8,128)S(1)} %copy-done.7, f32[768,8,384]{2,1,0:T(8,128)} %bitcast.278, f32[768,8,384]{2,1,0:T(8,128)} %bitcast.279), dimensions={2} | concatenate | bytes 56623104 | tf_op jit(solution)/shard_map/concatenate | solution.py:106
  746.5 25.3 %copy.155 = f32[96,8,8,1152]{3,1,2,0:T(8,128)} copy(f32[96,8,8,1152]{3,2,1,0:T(8,128)} %bitcast.271) | data formatting | bytes 56623104
  771.9 169.0 %reduce-scatter.3.cloned.1.call-done = f32[768,1152]{1,0:T(8,128)} async-done(((f32[768,9216]{1,0:T(8,128)}), f32[768,1152]{1,0:T(8,128)}) %reduce-scatter.3.cloned.1.call-update) | async-done | bytes 3538960 | tf_op jit(solution)/shard_map/reduce_scatter | solution.py:258
  944.3 75.6 %all-reduce.2.cloned.1.call-done = bf16[768,1152]{1,0:T(8,128)(2,1)} async-done(((bf16[768,1152]{1,0:T(8,128)(2,1)}), bf16[768,1152]{1,0:T(8,128)(2,1)}) %all-reduce.2.cloned.1.call-update) | async-done | bytes 1769488 | tf_op jit(solution)/shard_map/psum | solution.py:259
  1023.1 15.1 %fusion.77 = f32[768,2304]{0,1:T(8,128)} fusion(f32[288,768]{1,0:T(8,128)S(1)} %fusion.95, f32[1152,3072]{1,0:T(8,128)} %param.22), kind=kOutput, calls=%fused_computation.100 | convolution fusion | flops 6115295232 | bytes 10616832 | tf_op jit(solution)/shard_map/dot_general | solution.py:269
  1060.5 17.9 %fusion.71 = f32[768,3072]{1,0:T(8,128)S(1)} fusion(f32[384,768]{1,0:T(8,128)S(1)} %fusion.87, f32[1152,3072]{1,0:T(8,128)} %param.22), kind=kOutput, calls=%fused_computation.91 | convolution fusion | flops 10871635968 | bytes 15335424 | tf_op jit(solution)/shard_map/dot_general | solution.py:269
  1087.8 17.7 %fusion.67 = f32[768,3072]{1,0:T(8,128)S(1)} fusion(f32[384,768]{1,0:T(8,128)S(1)} %fusion.83, f32[1152,3072]{1,0:T(8,128)} %param.22), kind=kOutput, calls=%fused_computation.87 | convolution fusion | flops 10871635968 | bytes 15335424 | tf_op jit(solution)/shard_map/dot_general | solution.py:269
  1111.2 30.4 %concatenate.21 = f32[768,8,1152]{2,1,0:T(8,128)} concatenate(f32[768,8,288]{2,1,0:T(8,128)} %copy.137, f32[768,8,96]{2,1,0:T(8,128)S(1)} %copy.138, f32[768,8,384]{2,1,0:T(8,128)} %bitcast.280, f32[768,8,384]{2,1,0:T(8,128)} %bitcast.281), dimensions={2} | concatenate | bytes 56623104 | tf_op jit(solution)/shard_map/concatenate | solution.py:106
  1141.6 25.3 %copy.158 = f32[96,8,8,1152]{3,1,2,0:T(8,128)} copy(f32[96,8,8,1152]{3,2,1,0:T(8,128)} %bitcast.272) | data formatting | bytes 56623104
  1167.2 169.6 %reduce-scatter.5.cloned.1.call-done = f32[768,1152]{1,0:T(8,128)} async-done(((f32[768,9216]{1,0:T(8,128)}), f32[768,1152]{1,0:T(8,128)}) %reduce-scatter.5.cloned.1.call-update) | async-done | bytes 3538960 | tf_op jit(solution)/shard_map/reduce_scatter | solution.py:271
  1394.7 41.3 %psum.15 = f32[9216]{0:T(1024)} all-reduce(f32[9216]{0:T(1024)} %constant_dynamic-update-slice_fusion.6), channel_id=1, replica_groups=mesh['dp'=8,'seq'=4] {'dp','seq'}, use_global_device_ids=true, to_apply=%region_27.28 | all-reduce | flops 9216 | bytes 73728 | tf_op jit(solution)/shard_map/psum | solution.py:257
  (311 shorter events, 524.3 us)
Async XLA Ops:
  7.2 84.9 %all-gather.3.cloned.1.call-start = ((), (), s32[]{:S(2)}) async-start(), calls=%async_computation.10 | async-start | bytes 15925248 | tf_op jit(solution)/shard_map/all_gather | solution.py:110
  122.7 33.5 %all-to-all-start = ((bf16[3,256,4,192]{1,3,0,2:T(8,128)(2,1)}), bf16[3,256,4,192]{1,3,0,2:T(8,128)(2,1)S(1)}, u32[]{:S(2)}, u32[]{:S(2)}) async-start(bf16[3,256,4,192]{1,3,0,2:T(8,128)(2,1)} %copy.113), calls=%async_computation | async-start | bytes 2359296 | tf_op jit(solution)/shard_map/all_to_all | solution.py:137
  156.2 32.5 %all-to-all-start.1 = ((bf16[3,256,4,192]{1,3,0,2:T(8,128)(2,1)}), bf16[3,256,4,192]{1,3,0,2:T(8,128)(2,1)}, u32[]{:S(2)}, u32[]{:S(2)}) async-start(bf16[3,256,4,192]{1,3,0,2:T(8,128)(2,1)} %copy.115), calls=%async_computation.1 | async-start | bytes 2359296 | tf_op jit(solution)/shard_map/all_to_all | solution.py:135
  188.7 32.0 %all-to-all-start.2 = ((bf16[3,256,4,192]{1,3,0,2:T(8,128)(2,1)}), bf16[3,256,4,192]{1,3,0,2:T(8,128)(2,1)S(1)}, u32[]{:S(2)}, u32[]{:S(2)}) async-start(bf16[3,256,4,192]{1,3,0,2:T(8,128)(2,1)} %copy.117), calls=%async_computation.2 | async-start | bytes 2359296 | tf_op jit(solution)/shard_map/all_to_all | solution.py:136
  276.1 52.4 %all-to-all-start.3 = ((bf16[3,1024,1,192]{3,0,2,1:T(4,128)(2,1)}), bf16[3,1024,1,192]{3,0,2,1:T(4,128)(2,1)}, u32[]{:S(2)}, u32[]{:S(2)}) async-start(bf16[3,1024,1,192]{3,0,2,1:T(4,128)(2,1)} %copy.119), calls=%async_computation.3 | async-start | bytes 4194304 | tf_op jit(solution)/shard_map/all_to_all | solution.py:160
  338.2 32.2 %slice-start.8 = ((s8[4718592]{0:T(1024)(128)(4,1)}), s8[4194304]{0:T(1024)(128)(4,1)S(1)}, s32[]{:S(2)}) async-start(s8[4718592]{0:T(1024)(128)(4,1)} %bitcast.313), calls=%async_computation.23 | async-start | bytes 8388608
  341.6 56.9 %copy-start.3 = (f32[768,768]{1,0:T(8,128)}, f32[768,768]{1,0:T(8,128)S(1)}, u32[]{:S(2)}) copy-start(f32[768,768]{1,0:T(8,128)S(1)} %get-tuple-element.239) | copy-start | bytes 7077892
  341.6 56.8 %copy-start.26 = (f32[768]{0:T(1024)}, f32[768]{0:T(1024)S(1)}, u32[]{:S(2)}) copy-start(f32[768]{0:T(1024)S(1)} %broadcast_multiply_fusion.5) | copy-start | bytes 9220
  342.0 56.4 %copy-start.30 = (f32[768]{0:T(1024)}, f32[768]{0:T(1024)S(1)}, u32[]{:S(2)}) copy-start(f32[768]{0:T(1024)S(1)} %add_rsqrt_fusion.1) | copy-start | bytes 9220
  342.1 28.3 %slice-start.9 = ((s8[4718592]{0:T(1024)(128)(4,1)}), s8[524288]{0:T(1024)(128)(4,1)S(1)}, s32[]{:S(2)}) async-start(s8[4718592]{0:T(1024)(128)(4,1)} %bitcast.313), calls=%async_computation.24 | async-start | bytes 1048576
  529.4 51.7 %all-to-all-start.5 = ((bf16[3,1024,1,192]{3,0,2,1:T(4,128)(2,1)}), bf16[3,1024,1,192]{3,0,2,1:T(4,128)(2,1)}, u32[]{:S(2)}, u32[]{:S(2)}) async-start(bf16[3,1024,1,192]{3,0,2,1:T(4,128)(2,1)} %copy.124), calls=%async_computation.5 | async-start | bytes 4194304 | tf_op jit(solution)/shard_map/all_to_all | solution.py:227
  533.9 52.1 %copy-start.6 = (bf16[3,256,4,1,192]{4,2,1,0,3:T(4,128)(2,1)S(1)}, bf16[3,256,4,1,192]{4,2,1,0,3:T(4,128)(2,1)}, u32[]{:S(2)}) copy-start(bf16[3,256,4,1,192]{4,2,1,0,3:T(4,128)(2,1)} %copy-done.5) | copy-start | bytes 3538948
  581.1 52.7 %all-to-all-start.6 = ((bf16[3,1024,1,192]{3,0,2,1:T(4,128)(2,1)}), bf16[3,1024,1,192]{3,0,2,1:T(4,128)(2,1)}, u32[]{:S(2)}, u32[]{:S(2)}) async-start(bf16[3,1024,1,192]{3,0,2,1:T(4,128)(2,1)} %copy.127), calls=%async_computation.6 | async-start | bytes 4194304 | tf_op jit(solution)/shard_map/all_to_all | solution.py:228
  595.4 42.9 %copy-start.4 = (f32[768,768]{1,0:T(8,128)S(1)}, f32[768,768]{1,0:T(8,128)}, u32[]{:S(2)}) copy-start(f32[768,768]{1,0:T(8,128)} %copy-done.3) | copy-start | bytes 7077892
  595.4 42.9 %copy-start.27 = (f32[768]{0:T(1024)S(1)}, f32[768]{0:T(1024)}, u32[]{:S(2)}) copy-start(f32[768]{0:T(1024)} %copy-done.26) | copy-start | bytes 9220
  595.4 42.9 %copy-start.29 = (f32[768]{0:T(1024)S(1)}, f32[768]{0:T(1024)}, u32[]{:S(2)}) copy-start(f32[768]{0:T(1024)} %get-tuple-element.233) | copy-start | bytes 9220
  595.4 42.9 %copy-start.31 = (f32[768]{0:T(1024)S(1)}, f32[768]{0:T(1024)}, u32[]{:S(2)}) copy-start(f32[768]{0:T(1024)} %copy-done.30) | copy-start | bytes 9220
  595.4 42.9 %copy-start.33 = (f32[768]{0:T(1024)S(1)}, f32[768]{0:T(1024)}, u32[]{:S(2)}) copy-start(f32[768]{0:T(1024)} %get-tuple-element.232) | copy-start | bytes 9220
  633.8 52.3 %all-to-all-start.7 = ((bf16[3,1024,1,192]{3,0,2,1:T(4,128)(2,1)}), bf16[3,1024,1,192]{3,0,2,1:T(4,128)(2,1)}, u32[]{:S(2)}, u32[]{:S(2)}) async-start(bf16[3,1024,1,192]{3,0,2,1:T(4,128)(2,1)} %copy.130), calls=%async_computation.7 | async-start | bytes 4194304 | tf_op jit(solution)/shard_map/all_to_all | solution.py:229
  638.2 302.6 %reduce-scatter.3.cloned.1.call-start = ((), (), s32[]{:S(2)}) async-start(), calls=%async_computation.11 | async-start | bytes 31850496 | tf_op jit(solution)/shard_map/reduce_scatter | solution.py:258
  771.8 248.0 %all-reduce.2.cloned.1.call-start = ((), (), s32[]{:S(2)}) async-start(), calls=%async_computation.12 | async-start | bytes 3538944 | tf_op jit(solution)/shard_map/psum | solution.py:259
  944.2 392.6 %reduce-scatter.5.cloned.1.call-start = ((), (), s32[]{:S(2)}) async-start(), calls=%async_computation.13 | async-start | bytes 31850496 | tf_op jit(solution)/shard_map/reduce_scatter | solution.py:271
  1166.9 169.9 %copy-start.24 = (f32[768,1152]{1,0:T(8,128)S(1)}, f32[768,1152]{1,0:T(8,128)}, u32[]{:S(2)}) copy-start(f32[768,1152]{1,0:T(8,128)} %param.20) | copy-start | bytes 10616836
  1166.9 286.1 %all-gather.5.cloned.1.call-start = ((), (), s32[]{:S(2)}) async-start(), calls=%async_computation.14 | async-start | bytes 15925248 | tf_op jit(solution)/shard_map/all_gather | solution.py:284
  (47 other events, 379.9 us)
Sparse Core Ops, SparseCore 0:
  10.8 81.2 all-gather.2
  771.9 168.8 reduce-scatter.2
  944.4 75.4 all-reduce.1
  1167.1 169.7 reduce-scatter.4
  1373.1 79.8 all-gather.4
where the time goes:
time: 1520 us; the launch traced here: 1510 us
  waiting for transfers between devices  686 us (45%)
  local copies, waits for them, and re-layouts  334 us (22%)
  matrix products  287 us (19%)
  other arithmetic  80 us (5%)
  blocking collectives  72 us (5%)
  starting transfers between devices  31.7 us (2%)
    reduce_scatter x1, waiting for transfers between devices, on_device(): rotated = lax.psum_scatter(term, 'dp', scatter_dimension=1, tiled=True)  170 us
    reduce_scatter x1, waiting for transfers between devices, on_device(): reduced = lax.psum_scatter(grad_full, 'dp', scatter_dimension=1, tiled=True)  169 us
    unnamed x130, local copies, waits for them, and re-layouts  100 us
    all_gather x1, waiting for transfers between devices, on_device(): lax.all_gather(weights.astype(jnp.bfloat16), 'dp', axis=1, tiled=True)  80.8 us
    psum x1, waiting for transfers between devices, on_device(): reduced = lax.psum(reduced.astype(jnp.bfloat16), 'seq').astype(jnp.float32)  75.6 us
    concatenate x2, local copies, waits for them, and re-layouts, join_wide(): jnp.concatenate([parts[which].reshape(rows, owners, block_widths[which])...  60.8 us
    dot_general x4, matrix products, on_device(): turned_parts.append(jnp.dot(left_turned, rows_here, precision=highest))  55.1 us
    all_to_all x1, waiting for transfers between devices, on_device(): lax.all_to_all(to_send(grads_q), 'seq', split_axis=1, concat_axis=2, tile...  44.7 us
  transfers between devices with their start and end apart: 12, of which 12 were waited for; matrix products, arithmetic and copies ran while one was open for 8% of the time, Pallas kernels for 0%

commit v1 on v0

--- a/solution.py
+++ b/solution.py
@@ -256,7 +256,9 @@
     )
     small_grad = lax.psum(small_local, ("dp", "seq"))
     reduced = lax.psum_scatter(grad_full, "dp", scatter_dimension=1, tiled=True)
-    reduced = lax.psum(reduced.astype(jnp.bfloat16), "seq").astype(jnp.float32)
+    reduced = jnp.sum(lax.all_gather(reduced.astype(jnp.bfloat16), "seq"), axis=0).astype(
+        jnp.float32
+    )
     right_rows = []
     turned_parts = []
     for which in range(4):

time: 1520 us -> 1580 us (1.039)
  waiting for transfers between devices: 686 us -> 752 us
    all_gather x0 -> x1, waiting for transfers between devices: none -> 128 us  [on_device(): lax.all_gather(reduced.astype(jnp.bfloat16), 'seq')]
    psum x1 -> x0, waiting for transfers between devices: 75.6 us -> none  [on_device(): reduced = lax.psum(reduced.astype(jnp.bfloat16), 'seq').astype(jnp.float32)]
    unnamed x130 -> x142, local copies, waits for them, and re-layouts: 100 us -> 92.7 us
  transfers between devices with their start and end apart: 12 -> 12, of which waited for: 12 -> 12; matrix products, arithmetic and copies ran while one was open for 8% -> 7% of each run, Pallas kernels for 0% -> 0%
where the time goes in v1:
time: 1580 us; the launch traced here: 1570 us
  waiting for transfers between devices  752 us (48%)
  local copies, waits for them, and re-layouts  325 us (21%)
  matrix products  288 us (18%)
  other arithmetic  82 us (5%)
  blocking collectives  71.7 us (5%)
  starting transfers between devices  31.6 us (2%)
    reduce_scatter x1, waiting for transfers between devices, on_device(): reduced = lax.psum_scatter(grad_full, 'dp', scatter_dimension=1, tiled=True)  169 us
    reduce_scatter x1, waiting for transfers between devices, on_device(): rotated = lax.psum_scatter(term, 'dp', scatter_dimension=1, tiled=True)  169 us
    all_gather x1, waiting for transfers between devices, on_device(): lax.all_gather(reduced.astype(jnp.bfloat16), 'seq')  128 us
    unnamed x142, local copies, waits for them, and re-layouts  92.7 us
    all_gather x1, waiting for transfers between devices, on_device(): lax.all_gather(weights.astype(jnp.bfloat16), 'dp', axis=1, tiled=True)  80.8 us
    concatenate x2, local copies, waits for them, and re-layouts, join_wide(): jnp.concatenate([parts[which].reshape(rows, owners, block_widths[which])...  61.4 us
    dot_general x4, matrix products, on_device(): turned_parts.append(jnp.dot(left_turned, rows_here, precision=highest))  55.5 us
    all_to_all x1, waiting for transfers between devices, on_device(): lax.all_to_all(to_send(grads_q), 'seq', split_axis=1, concat_axis=2, tile...  44.8 us
  transfers between devices with their start and end apart: 12, of which 12 were waited for; matrix products, arithmetic and copies ran while one was open for 7% of the time, Pallas kernels for 0%

profile of v1, /device:TPU:0, one launch (start us, length us, event | category | flops | bytes accessed | tf_op | source)
XLA Modules:
  0.0 1565.8 jit_solution(12672901740985369222)
XLA Ops:
  11.3 80.8 %all-gather.5.cloned.1.call-done = bf16[768,9216]{1,0:T(8,128)(2,1)} async-done(((bf16[768,1152]{1,0:T(8,128)(2,1)}), bf16[768,9216]{1,0:T(8,128)(2,1)}) %all-gather.5.cloned.1.call-update) | async-done | bytes 14155792 | tf_op jit(solution)/shard_map/all_gather | solution.py:110
  92.1 18.6 %copy.112 = bf16[768,9216]{0,1:T(8,128)(2,1)} copy(bf16[768,9216]{1,0:T(8,128)(2,1)} %all-gather.5.cloned.1.call-done) | data formatting | bytes 28311552 | tf_op jit(solution)/shard_map/all_gather | solution.py:110
  132.9 23.3 %all-to-all-done = bf16[3,256,4,192]{1,3,0,2:T(8,128)(2,1)S(1)} async-done(((bf16[3,256,4,192]{1,3,0,2:T(8,128)(2,1)}), bf16[3,256,4,192]{1,3,0,2:T(8,128)(2,1)S(1)}, u32[]{:S(2)}, u32[]{:S(2)}) %all-to-all-start) | async-done | bytes 1179680 | tf_op jit(solution)/shard_map/all_to_all | solution.py:137
  169.0 19.7 %all-to-all-done.1 = bf16[3,256,4,192]{1,3,0,2:T(8,128)(2,1)} async-done(((bf16[3,256,4,192]{1,3,0,2:T(8,128)(2,1)}), bf16[3,256,4,192]{1,3,0,2:T(8,128)(2,1)}, u32[]{:S(2)}, u32[]{:S(2)}) %all-to-all-start.1) | async-done | bytes 1179680 | tf_op jit(solution)/shard_map/all_to_all | solution.py:135
  201.9 18.9 %all-to-all-done.2 = bf16[3,256,4,192]{1,3,0,2:T(8,128)(2,1)S(1)} async-done(((bf16[3,256,4,192]{1,3,0,2:T(8,128)(2,1)}), bf16[3,256,4,192]{1,3,0,2:T(8,128)(2,1)S(1)}, u32[]{:S(2)}, u32[]{:S(2)}) %all-to-all-start.2) | async-done | bytes 1179680 | tf_op jit(solution)/shard_map/all_to_all | solution.py:136
  224.5 47.5 %while.26 = (s32[]{:T(128)}, bf16[3,1024,3,64]{1,3,2,0:T(8,128)(2,1)}, f32[3,3,1024,1]{2,1,3,0:T(4,128)}, bf16[3,1024,3,64]{1,3,2,0:T(8,128)(2,1)}, s32[3,1024]{...) while((s32[]{:T(128)}, ...), condition=%wide.region_3.4_spmd, body=%wide.region_0.3_spmd.sunk | while | flops 844297216 | bytes 47827072 | solution.py:158
  293.2 35.4 %all-to-all-done.3 = bf16[3,1024,1,192]{3,0,2,1:T(4,128)(2,1)} async-done(((bf16[3,1024,1,192]{3,0,2,1:T(4,128)(2,1)}), bf16[3,1024,1,192]{3,0,2,1:T(4,128)(2,1)}, u32[]{:S(2)}, u32[]{:S(2)}) %all-to-all-start.3) | async-done | bytes 1179680 | tf_op jit(solution)/shard_map/all_to_all | solution.py:160
  342.1 28.3 %multiply_convert_fusion.1 = (bf16[768,3072]{1,0:T(8,128)(2,1)S(1)}, f32[768,3072]{1,0:T(8,128)}, f32[768,3072]{1,0:T(8,128)}) fusion(f32[3072]{0:T(1024)S(1)} %slice.124, bf16[768,3072]{0,1:T(8,128)(2,1)} %bitcast.310, f32[768,768]{1,0:T(8,128)S(1)} %get-tuple-element.239, f32[768]{0:T(1024)S(1)} %copy-done.31, f32[768]{0:T(1024)S(1)} %copy-done.27, ...), kind=kOutput, calls=%fused_computation.70 | convolution fusion | flops 3782541312 | bytes 30695424 | tf_op jit(solution)/shard_map/dot_general | solution.py:166
  405.0 30.7 %all_to_all.120 = bf16[3,256,4,192]{1,3,0,2:T(8,128)(2,1)S(1)} all-to-all(bf16[3,256,4,192]{1,3,0,2:T(8,128)(2,1)S(1)} %copy.122), channel_id=1, replica_groups=mesh['dp'=8,'seq'=4] {'seq'}, dimensions={2} | all-to-all | bytes 2359296 | tf_op jit(solution)/shard_map/all_to_all | solution.py:191
  443.9 81.4 %while.27 = (s32[]{:T(128)}, bf16[3,1024,3,64]{1,3,2,0:T(8,128)(2,1)}, bf16[3,1024,3,64]{1,3,2,0:T(8,128)(2,1)}, bf16[3,1024,3,64]{1,3,2,0:T(8,128)(2,1)}, bf16[...) while((s32[]{:T(128)}, ...), condition=%wide.region_14.15_spmd, body=%wide.region_12.14_spmd.sunk | while | flops 2062480384 | bytes 102610048 | solution.py:219
  536.4 44.8 %all-to-all-done.5 = bf16[3,1024,1,192]{3,0,2,1:T(4,128)(2,1)} async-done(((bf16[3,1024,1,192]{3,0,2,1:T(4,128)(2,1)}), bf16[3,1024,1,192]{3,0,2,1:T(4,128)(2,1)}, u32[]{:S(2)}, u32[]{:S(2)}) %all-to-all-start.5) | async-done | bytes 1179680 | tf_op jit(solution)/shard_map/all_to_all | solution.py:227
  597.8 35.8 %all-to-all-done.6 = bf16[3,1024,1,192]{3,0,2,1:T(4,128)(2,1)} async-done(((bf16[3,1024,1,192]{3,0,2,1:T(4,128)(2,1)}), bf16[3,1024,1,192]{3,0,2,1:T(4,128)(2,1)}, u32[]{:S(2)}, u32[]{:S(2)}) %all-to-all-start.6) | async-done | bytes 1179680 | tf_op jit(solution)/shard_map/all_to_all | solution.py:228
  715.9 30.4 %concatenate.20 = f32[768,8,1152]{2,1,0:T(8,128)} concatenate(f32[768,8,288]{2,1,0:T(8,128)} %copy.134, f32[768,8,96]{2,1,0:T(8,128)S(1)} %copy-done.8, f32[768,8,384]{2,1,0:T(8,128)} %bitcast.279, f32[768,8,384]{2,1,0:T(8,128)} %bitcast.280), dimensions={2} | concatenate | bytes 56623104 | tf_op jit(solution)/shard_map/concatenate | solution.py:106
  746.3 25.3 %copy.155 = f32[96,8,8,1152]{3,1,2,0:T(8,128)} copy(f32[96,8,8,1152]{3,2,1,0:T(8,128)} %bitcast.272) | data formatting | bytes 56623104
  771.7 168.9 %reduce-scatter.3.cloned.1.call-done = f32[768,1152]{1,0:T(8,128)} async-done(((f32[768,9216]{1,0:T(8,128)}), f32[768,1152]{1,0:T(8,128)}) %reduce-scatter.3.cloned.1.call-update) | async-done | bytes 3538960 | tf_op jit(solution)/shard_map/reduce_scatter | solution.py:258
  944.3 128.1 %all-gather.9.cloned.1.call-done = bf16[3072,1152]{1,0:T(8,128)(2,1)} async-done(((bf16[768,1152]{1,0:T(8,128)(2,1)}), bf16[3072,1152]{1,0:T(8,128)(2,1)}) %all-gather.9.cloned.1.call-update) | async-done | bytes 7077904 | tf_op jit(solution)/shard_map/all_gather | solution.py:259
  1091.1 15.1 fusion.77
  1123.0 18.3 %fusion.71 = f32[768,3072]{1,0:T(8,128)S(1)} fusion(f32[384,768]{1,0:T(8,128)} %fusion.87, f32[1152,3072]{1,0:T(8,128)} %param.22), kind=kOutput, calls=%fused_computation.91 | convolution fusion | flops 10871635968 | bytes 15335424 | tf_op jit(solution)/shard_map/dot_general | solution.py:271
  1147.1 17.7 %fusion.67 = f32[768,3072]{1,0:T(8,128)S(1)} fusion(f32[384,768]{1,0:T(8,128)S(1)} %fusion.83, f32[1152,3072]{1,0:T(8,128)} %param.22), kind=kOutput, calls=%fused_computation.87 | convolution fusion | flops 10871635968 | bytes 15335424 | tf_op jit(solution)/shard_map/dot_general | solution.py:271
  1170.6 31.0 %concatenate.21 = f32[768,8,1152]{2,1,0:T(8,128)} concatenate(f32[768,8,288]{2,1,0:T(8,128)} %copy.137, f32[768,8,96]{2,1,0:T(8,128)} %copy.138, f32[768,8,384]{2,1,0:T(8,128)} %bitcast.281, f32[768,8,384]{2,1,0:T(8,128)} %bitcast.282), dimensions={2} | concatenate | bytes 56623104 | tf_op jit(solution)/shard_map/concatenate | solution.py:106
  1201.6 25.3 %copy.158 = f32[96,8,8,1152]{3,1,2,0:T(8,128)} copy(f32[96,8,8,1152]{3,2,1,0:T(8,128)} %bitcast.273) | data formatting | bytes 56623104
  1227.2 168.8 %reduce-scatter.5.cloned.1.call-done = f32[768,1152]{1,0:T(8,128)} async-done(((f32[768,9216]{1,0:T(8,128)}), f32[768,1152]{1,0:T(8,128)}) %reduce-scatter.5.cloned.1.call-update) | async-done | bytes 3538960 | tf_op jit(solution)/shard_map/reduce_scatter | solution.py:273
  1441.6 41.0 %psum.7 = f32[9216]{0:T(1024)S(1)} all-reduce(f32[9216]{0:T(1024)S(1)} %constant_dynamic-update-slice_fusion.6), channel_id=1, replica_groups=mesh['dp'=8,'seq'=4] {'dp','seq'}, use_global_device_ids=true, to_apply=%region_27.28 | all-reduce | flops 9216 | bytes 73728 | tf_op jit(solution)/shard_map/psum | solution.py:257
  1493.1 20.2 %all-gather.7.cloned.1.call-done = bf16[768,9216]{0,1:T(8,128)(2,1)} async-done(((bf16[768,1152]{0,1:T(8,128)(2,1)}), bf16[768,9216]{0,1:T(8,128)(2,1)}) %all-gather.7.cloned.1.call-update) | async-done | bytes 14155792 | tf_op jit(solution)/shard_map/all_gather | solution.py:286
  (324 shorter events, 524.1 us)
Async XLA Ops:
  7.2 84.9 %all-gather.5.cloned.1.call-start = ((), (), s32[]{:S(2)}) async-start(), calls=%async_computation.10 | async-start | bytes 15925248 | tf_op jit(solution)/shard_map/all_gather | solution.py:110
  122.7 33.6 %all-to-all-start = ((bf16[3,256,4,192]{1,3,0,2:T(8,128)(2,1)}), bf16[3,256,4,192]{1,3,0,2:T(8,128)(2,1)S(1)}, u32[]{:S(2)}, u32[]{:S(2)}) async-start(bf16[3,256,4,192]{1,3,0,2:T(8,128)(2,1)} %copy.113), calls=%async_computation | async-start | bytes 2359296 | tf_op jit(solution)/shard_map/all_to_all | solution.py:137
  156.3 32.4 %all-to-all-start.1 = ((bf16[3,256,4,192]{1,3,0,2:T(8,128)(2,1)}), bf16[3,256,4,192]{1,3,0,2:T(8,128)(2,1)}, u32[]{:S(2)}, u32[]{:S(2)}) async-start(bf16[3,256,4,192]{1,3,0,2:T(8,128)(2,1)} %copy.115), calls=%async_computation.1 | async-start | bytes 2359296 | tf_op jit(solution)/shard_map/all_to_all | solution.py:135
  188.7 32.0 %all-to-all-start.2 = ((bf16[3,256,4,192]{1,3,0,2:T(8,128)(2,1)}), bf16[3,256,4,192]{1,3,0,2:T(8,128)(2,1)S(1)}, u32[]{:S(2)}, u32[]{:S(2)}) async-start(bf16[3,256,4,192]{1,3,0,2:T(8,128)(2,1)} %copy.117), calls=%async_computation.2 | async-start | bytes 2359296 | tf_op jit(solution)/shard_map/all_to_all | solution.py:136
  276.1 52.5 %all-to-all-start.3 = ((bf16[3,1024,1,192]{3,0,2,1:T(4,128)(2,1)}), bf16[3,1024,1,192]{3,0,2,1:T(4,128)(2,1)}, u32[]{:S(2)}, u32[]{:S(2)}) async-start(bf16[3,1024,1,192]{3,0,2,1:T(4,128)(2,1)} %copy.119), calls=%async_computation.3 | async-start | bytes 4194304 | tf_op jit(solution)/shard_map/all_to_all | solution.py:160
  341.6 56.9 %copy-start.3 = (f32[768,768]{1,0:T(8,128)}, f32[768,768]{1,0:T(8,128)S(1)}, u32[]{:S(2)}) copy-start(f32[768,768]{1,0:T(8,128)S(1)} %get-tuple-element.239) | copy-start | bytes 7077892
  341.7 56.8 %copy-start.25 = (f32[768]{0:T(1024)}, f32[768]{0:T(1024)S(1)}, u32[]{:S(2)}) copy-start(f32[768]{0:T(1024)S(1)} %broadcast_multiply_fusion.5) | copy-start | bytes 9220
  342.1 56.4 %copy-start.29 = (f32[768]{0:T(1024)}, f32[768]{0:T(1024)S(1)}, u32[]{:S(2)}) copy-start(f32[768]{0:T(1024)S(1)} %add_rsqrt_fusion.1) | copy-start | bytes 9220
  529.4 51.7 %all-to-all-start.5 = ((bf16[3,1024,1,192]{3,0,2,1:T(4,128)(2,1)}), bf16[3,1024,1,192]{3,0,2,1:T(4,128)(2,1)}, u32[]{:S(2)}, u32[]{:S(2)}) async-start(bf16[3,1024,1,192]{3,0,2,1:T(4,128)(2,1)} %copy.124), calls=%async_computation.5 | async-start | bytes 4194304 | tf_op jit(solution)/shard_map/all_to_all | solution.py:227
  533.9 51.9 %copy-start.7 = (bf16[3,256,4,1,192]{4,2,1,0,3:T(4,128)(2,1)S(1)}, bf16[3,256,4,1,192]{4,2,1,0,3:T(4,128)(2,1)}, u32[]{:S(2)}) copy-start(bf16[3,256,4,1,192]{4,2,1,0,3:T(4,128)(2,1)} %copy-done.6) | copy-start | bytes 3538948
  581.2 52.5 %all-to-all-start.6 = ((bf16[3,1024,1,192]{3,0,2,1:T(4,128)(2,1)}), bf16[3,1024,1,192]{3,0,2,1:T(4,128)(2,1)}, u32[]{:S(2)}, u32[]{:S(2)}) async-start(bf16[3,1024,1,192]{3,0,2,1:T(4,128)(2,1)} %copy.127), calls=%async_computation.6 | async-start | bytes 4194304 | tf_op jit(solution)/shard_map/all_to_all | solution.py:228
  595.2 42.9 %copy-start.4 = (f32[768,768]{1,0:T(8,128)S(1)}, f32[768,768]{1,0:T(8,128)}, u32[]{:S(2)}) copy-start(f32[768,768]{1,0:T(8,128)} %copy-done.3) | copy-start | bytes 7077892
  595.2 42.9 %copy-start.26 = (f32[768]{0:T(1024)S(1)}, f32[768]{0:T(1024)}, u32[]{:S(2)}) copy-start(f32[768]{0:T(1024)} %copy-done.25) | copy-start | bytes 9220
  595.2 42.9 %copy-start.28 = (f32[768]{0:T(1024)S(1)}, f32[768]{0:T(1024)}, u32[]{:S(2)}) copy-start(f32[768]{0:T(1024)} %get-tuple-element.233) | copy-start | bytes 9220
  595.2 42.9 %copy-start.30 = (f32[768]{0:T(1024)S(1)}, f32[768]{0:T(1024)}, u32[]{:S(2)}) copy-start(f32[768]{0:T(1024)} %copy-done.29) | copy-start | bytes 9220
  595.2 42.9 %copy-start.32 = (f32[768]{0:T(1024)S(1)}, f32[768]{0:T(1024)}, u32[]{:S(2)}) copy-start(f32[768]{0:T(1024)} %get-tuple-element.232) | copy-start | bytes 9220
  633.6 52.3 %all-to-all-start.7 = ((bf16[3,1024,1,192]{3,0,2,1:T(4,128)(2,1)}), bf16[3,1024,1,192]{3,0,2,1:T(4,128)(2,1)}, u32[]{:S(2)}, u32[]{:S(2)}) async-start(bf16[3,1024,1,192]{3,0,2,1:T(4,128)(2,1)} %copy.130), calls=%async_computation.7 | async-start | bytes 4194304 | tf_op jit(solution)/shard_map/all_to_all | solution.py:229
  638.1 302.5 %reduce-scatter.3.cloned.1.call-start = ((), (), s32[]{:S(2)}) async-start(), calls=%async_computation.11 | async-start | bytes 31850496 | tf_op jit(solution)/shard_map/reduce_scatter | solution.py:258
  771.6 300.7 %all-gather.9.cloned.1.call-start = ((), (), s32[]{:S(2)}) async-start(), calls=%async_computation.14 | async-start | bytes 8847360 | tf_op jit(solution)/shard_map/all_gather | solution.py:259
  944.0 452.0 %reduce-scatter.5.cloned.1.call-start = ((), (), s32[]{:S(2)}) async-start(), calls=%async_computation.12 | async-start | bytes 31850496 | tf_op jit(solution)/shard_map/reduce_scatter | solution.py:273
  1227.0 286.4 %all-gather.7.cloned.1.call-start = ((), (), s32[]{:S(2)}) async-start(), calls=%async_computation.13 | async-start | bytes 15925248 | tf_op jit(solution)/shard_map/all_gather | solution.py:286
  1433.3 49.3 %copy-start.34 = (f32[9216]{0:T(1024)S(1)}, f32[9216]{0:T(1024)}, u32[]{:S(2)}) copy-start(f32[9216]{0:T(1024)} %param.23) | copy-start | bytes 110596
  1433.3 49.3 %copy-start.38 = (f32[9216]{0:T(1024)S(1)}, f32[9216]{0:T(1024)}, u32[]{:S(2)}) copy-start(f32[9216]{0:T(1024)} %param.25) | copy-start | bytes 110596
  1433.3 49.3 %copy-start.39 = (f32[9216]{0:T(1024)S(1)}, f32[9216]{0:T(1024)}, u32[]{:S(2)}) copy-start(f32[9216]{0:T(1024)} %param.24) | copy-start | bytes 110596
  (53 other events, 450.7 us)
Sparse Core Ops, SparseCore 0:
  10.8 81.2 all-gather.4
  771.8 168.8 reduce-scatter.2
  944.2 128.1 all-gather.8
  1227.1 168.8 reduce-scatter.4
  1433.3 79.9 all-gather.6
